TPU v7x, 32 devices: a whole 2x2x4 slice. The times are simulated.
32 devices in a mesh: grp: 4 (over x, core), ctx: 8 (over z, y).
Axes of the slice: x: 2, y: 2, z: 4, core: 2. Of those that a mesh axis runs over, the one named last changes fastest.
Arguments:
- queries: bfloat16 [4096, 4096], P(('grp', 'ctx')), parts along dimension 0, may hold values from -8 to 8
- key_states: bfloat16 [4096, 512], P(('grp', 'ctx')), parts along dimension 0, may hold values from -8 to 8
- value_states: bfloat16 [4096, 512], P(('grp', 'ctx')), parts along dimension 0, may hold values from -6 to 6
- grads_out: bfloat16 [4096, 4096], P(('grp', 'ctx')), parts along dimension 0, may hold values from -6 to 6
- doc_lengths: int32 [32], P('grp'), parts along dimension 0, may hold values from 1 to 256, as said below
- block_plan: int32 [64], P('grp'), parts along dimension 0, may hold values from 0 to 15, as said below
- needed: int32 [32, 2], P('grp'), parts along dimension 0, may hold values from 0 to 15, as said below
Outputs:
- outputs: bfloat16 [4096, 4096], P(('grp', 'ctx')), parts along dimension 0
- query_grads: bfloat16 [4096, 4096], P(('grp', 'ctx')), parts along dimension 0
- key_grads: bfloat16 [4096, 512], P(('grp', 'ctx')), parts along dimension 0
- value_grads: bfloat16 [4096, 512], P(('grp', 'ctx')), parts along dimension 0
There are 4 independent parts, one for each index of `grp`. A program takes and returns all parts, laid end to end along the dimension named above; each array names one. Nothing has to cross between parts.
Inputs may be any that keep to these rules, and one draw needn't show every extreme that they name: `doc_lengths`: the lengths sum to 1024 and one of them is exactly 256. `block_plan`: each block position appears once. `needed`: each row lists 2 different stored block numbers, no two of which have the same value of block number // 2.
All inputs are finite; a program needn't handle non-finite values.
Results may differ from a plain program's by a relative error of at most 0.013.
Values may be sent and summed in bfloat16 or wider, within the bound.
A program may use at most 128 MiB of HBM per device.

v0:
```python
import functools
import math

import jax
import jax.numpy as jnp
from jax import lax
from jax.experimental import pallas as pl
from jax.experimental.pallas import tpu as pltpu
from jax.sharding import PartitionSpec as P

HEADS = 32
KV_HEADS = 4
HEAD_DIM = 128
BLK = 64
GROUP = HEADS // KV_HEADS
CHUNKS = 2
PER_CHUNK = KV_HEADS // CHUNKS
WIDE = 2 * HEAD_DIM * PER_CHUNK
PAIR = 2

masked_score = -1e30


def matmul(a, b, contract):
    return lax.dot_general(
        a, b, ((contract[:1], contract[1:]), ((), ())), preferred_element_type=jnp.float32
    )


def kernel(n, q_hbm, k_ref, v_ref, do_hbm, doc_ref, plan_ref, need_ref, *rest):
    out_hbm, dq_hbm, dk_ref, dv_ref = rest[:4]
    q_buf, do_buf, out_buf, dq_buf, key_acc, value_acc, bias = rest[4:11]
    send, grad_send, grad_recv = rest[11:14]
    recv = rest[14 : 14 + CHUNKS]
    relayed = rest[14 + CHUNKS : 14 + 2 * CHUNKS]
    grad_parts = rest[14 + 2 * CHUNKS : 14 + 3 * CHUNKS]
    grad_relayed = rest[14 + 3 * CHUNKS : 14 + 4 * CHUNKS]
    whole = rest[14 + 4 * CHUNKS]
    fwd_send, fwd_recv, bwd_send, bwd_recv, load_sem, store_sem = rest[15 + 4 * CHUNKS :]
    rows = q_buf.shape[0]
    own_blocks = rows // BLK
    listed_count = need_ref.shape[1]
    me = lax.axis_index("ctx")
    side = n // 2
    local = lax.rem(me, side)
    side_start = me - local
    partner = lax.rem(me + side, n)
    score_scale = 1.0 / math.sqrt(HEAD_DIM)
    chunk_cols = PER_CHUNK * GROUP * HEAD_DIM

    def cols(c):
        return pl.ds(c * chunk_cols, chunk_cols)

    loads, stores, fetches, returns = {}, {}, {}, {}
    for c in range(CHUNKS):
        for i, (src, dst) in enumerate(((q_hbm, q_buf), (do_hbm, do_buf))):
            loads[i, c] = pltpu.make_async_copy(
                src.at[:, cols(c)], dst.at[:, cols(c)], load_sem.at[i, c]
            )
            loads[i, c].start()

    barrier = pltpu.get_barrier_semaphore()
    for o in range(1, n):
        pl.semaphore_signal(
            barrier,
            inc=1,
            device_id={"ctx": lax.rem(me + o, n)},
            device_id_type=pl.DeviceIdType.MESH,
        )

    def near(o):
        return side_start + lax.rem(local + o, side)

    def half_for(peer, owner):
        half = jnp.int32(0)
        for j in range(listed_count):
            block = need_ref[peer, j]
            half = jnp.where(block // own_blocks == owner, block % own_blocks, half)
        return half

    def pack(keys, values, c):
        pieces = []
        for i in range(PER_CHUNK):
            g = c * PER_CHUNK + i
            at = slice(g * HEAD_DIM, (g + 1) * HEAD_DIM)
            pieces += [keys[:, at], values[:, at]]
        return jnp.concatenate(pieces, axis=1)

    def fetch(key, src, dst, peer, slot, c):
        fetches[key] = pltpu.make_async_remote_copy(
            src_ref=src,
            dst_ref=dst,
            send_sem=fwd_send.at[slot, c],
            recv_sem=fwd_recv.at[slot, c],
            device_id={"ctx": peer},
            device_id_type=pl.DeviceIdType.MESH,
        )
        fetches[key].start()

    for c in range(CHUNKS):
        for b in range(own_blocks):
            whole[c, b] = pack(k_ref[b], v_ref[b], c)
    for o in range(1, side):
        half = half_for(near(o), me)
        keys, values = k_ref[half], v_ref[half]
        for c in range(CHUNKS):
            send[o, c] = pack(keys, values, c)
    for c in range(CHUNKS):
        recv[c][0] = jnp.zeros((BLK, WIDE), jnp.bfloat16)

    pl.semaphore_wait(barrier, n - 1)
    for c in range(CHUNKS):
        fetch((0, c), whole.at[c], relayed[c], partner, 0, c)
    for c in range(CHUNKS):
        for o in range(1, side):
            fetch((o, c), send.at[o, c], recv[c].at[o], near(o), o, c)

    ends, total = [], jnp.int32(0)
    for d in range(doc_ref.shape[0]):
        total = total + doc_ref[d]
        ends.append(total)

    def documents(place):
        doc = jnp.zeros_like(place)
        for end in ends:
            doc = doc + (place >= end).astype(jnp.int32)
        return doc

    key_row = lax.broadcasted_iota(jnp.int32, (BLK, rows), 0)
    query_col = lax.broadcasted_iota(jnp.int32, (BLK, rows), 1)
    query_local = query_col // BLK
    query_place = query_col
    for b in range(own_blocks):
        shift = (plan_ref[me * own_blocks + b] - b) * BLK
        query_place = jnp.where(query_local == b, query_col + shift, query_place)
    query_doc = documents(query_place)
    listed = [need_ref[me, j] for j in range(listed_count)]
    for s in range(own_blocks + listed_count):
        if s < own_blocks:
            block = me * own_blocks + s
            found = jnp.int32(0)
            for b in listed:
                found = jnp.where(b == block, 1, found)
            allowed = jnp.where(query_local == s, 1, found)
        else:
            block = listed[s - own_blocks]
            allowed = jnp.where(block // own_blocks == me, 0, jnp.ones_like(query_col))
        key_place = key_row + plan_ref[block] * BLK
        visible = (allowed > 0) & (documents(key_place) == query_doc) & (key_place <= query_place)
        bias[s * BLK : (s + 1) * BLK, :] = jnp.where(visible, 0.0, masked_score)

    for c in range(CHUNKS):
        fetches[0, c].wait_recv()
        for o in range(1, side):
            send[side + o, c] = relayed[c][half_for(near(o), partner)]
            fetch((side + o, c), send.at[side + o, c], recv[c].at[side + o], near(o), side + o, c)
        recv[c][side] = relayed[c][half_for(me, partner)]

    def part_for(requester, owner):
        part = jnp.int32(0)
        for j in range(listed_count):
            part = jnp.where(need_ref[requester, j] // own_blocks == owner, j, part)
        return part

    def send_back(key, src, dst, peer, slot, c):
        returns[key] = pltpu.make_async_remote_copy(
            src_ref=src,
            dst_ref=dst,
            send_sem=bwd_send.at[slot, c],
            recv_sem=bwd_recv.at[slot, c],
            device_id={"ctx": peer},
            device_id_type=pl.DeviceIdType.MESH,
        )
        returns[key].start()

    slots = []
    for b in listed:
        owner = b // own_blocks
        owner_local = owner % side
        apart = jnp.where(owner - owner_local == side_start, 0, side)
        slots.append(lax.rem(local - owner_local + side, side) + apart)
    exponent = score_scale * math.log2(math.e)

    for c in range(CHUNKS):
        loads[0, c].wait()
        loads[1, c].wait()
        for o in range(1, n):
            if o != side:
                fetches[o, c].wait_recv()
        arrived = [recv[c][slot] for slot in slots]
        for i in range(PER_CHUNK):
            g = c * PER_CHUNK + i
            own_at = slice(g * HEAD_DIM, (g + 1) * HEAD_DIM)
            base = 2 * i * HEAD_DIM
            keys = jnp.concatenate(
                [k_ref[b, :, own_at] for b in range(own_blocks)]
                + [piece[:, base : base + HEAD_DIM] for piece in arrived],
                axis=0,
            )
            values = jnp.concatenate(
                [v_ref[b, :, own_at] for b in range(own_blocks)]
                + [piece[:, base + HEAD_DIM : base + 2 * HEAD_DIM] for piece in arrived],
                axis=0,
            )
            keys_t, values_t = keys.T, values.T
            key_grad = value_grad = None
            for p in range(GROUP // PAIR):
                heads = [
                    slice((g * GROUP + p * PAIR + x) * HEAD_DIM, (g * GROUP + p * PAIR + x + 1) * HEAD_DIM)
                    for x in range(PAIR)
                ]
                queries = jnp.concatenate([q_buf[:, at] for at in heads], axis=0)
                grads = jnp.concatenate([do_buf[:, at] for at in heads], axis=0)
                mask = bias[...]
                scores = matmul(keys, queries, (1, 1)) + jnp.concatenate([mask] * PAIR, axis=1)
                highest = jnp.max(scores, axis=0, keepdims=True)
                weights = jnp.exp2((scores - highest) * exponent)
                weights = weights * (1.0 / jnp.sum(weights, axis=0, keepdims=True))
                low = weights.astype(jnp.bfloat16)
                attended = matmul(values_t, low, (1, 0)).T.astype(jnp.bfloat16)
                prob_grads = matmul(values, grads, (1, 1))
                delta = jnp.sum(weights * prob_grads, axis=0, keepdims=True)
                score_grads = (weights * (prob_grads - delta)).astype(jnp.bfloat16)
                query_grad = (matmul(keys_t, score_grads, (1, 0)) * score_scale).T
                query_grad = query_grad.astype(jnp.bfloat16)
                for x, at in enumerate(heads):
                    out_buf[:, at] = attended[x * rows : (x + 1) * rows]
                    dq_buf[:, at] = query_grad[x * rows : (x + 1) * rows]
                more_keys = matmul(score_grads, queries, (1, 0))
                more_values = matmul(low, grads, (1, 0))
                key_grad = more_keys if key_grad is None else key_grad + more_keys
                value_grad = more_values if value_grad is None else value_grad + more_values
            key_grad = key_grad * score_scale
            key_acc[:, own_at] = key_grad[:rows]
            value_acc[:, own_at] = value_grad[:rows]
            for grad, at in ((key_grad, base), (value_grad, base + HEAD_DIM)):
                for j in range(listed_count):
                    first = rows + j * BLK
                    grad_parts[c][j, :, at : at + HEAD_DIM] = grad[first : first + BLK].astype(
                        jnp.bfloat16
                    )
        send_back((0, c), grad_parts[c], grad_relayed[c], partner, 0, c)
        for o in range(1, side):
            owner = near(side - o)
            grad_send[o, c] = grad_parts[c][part_for(me, owner)]
            send_back((o, c), grad_send.at[o, c], grad_recv.at[o, c], owner, o, c)
        for i, (src, dst) in enumerate(((out_buf, out_hbm), (dq_buf, dq_hbm))):
            stores[i, c] = pltpu.make_async_copy(
                src.at[:, cols(c)], dst.at[:, cols(c)], store_sem.at[i, c]
            )
            stores[i, c].start()

    for c in range(CHUNKS):
        returns[0, c].wait_recv()
        for o in range(1, side):
            owner, slot = near(side - o), side + o
            grad_send[slot, c] = grad_relayed[c][part_for(partner, owner)]
            send_back((slot, c), grad_send.at[slot, c], grad_recv.at[slot, c], owner, slot, c)
        grad_recv[side, c] = grad_relayed[c][part_for(partner, me)]

    for c in range(CHUNKS):
        for o in range(1, n):
            if o != side:
                returns[o, c].wait_recv()
        for i in range(PER_CHUNK):
            g = c * PER_CHUNK + i
            own_at = slice(g * HEAD_DIM, (g + 1) * HEAD_DIM)
            base = 2 * i * HEAD_DIM
            for acc, result, at in ((key_acc, dk_ref, base), (value_acc, dv_ref, base + HEAD_DIM)):
                sums = [acc[b * BLK : (b + 1) * BLK, own_at] for b in range(own_blocks)]
                for o in range(1, n):
                    peer = near(o) if o < side else lax.rem(near(o - side) + side, n)
                    part = grad_recv[o, c, :, at : at + HEAD_DIM].astype(jnp.float32)
                    for b in range(own_blocks):
                        hit = jnp.int32(0)
                        for j in range(listed_count):
                            hit = jnp.where(need_ref[peer, j] == me * own_blocks + b, 1, hit)
                        sums[b] = sums[b] + jnp.where(hit > 0, part, 0.0)
                for b in range(own_blocks):
                    result[b * BLK : (b + 1) * BLK, own_at] = sums[b].astype(jnp.bfloat16)
    for c in range(CHUNKS):
        for o in range(n):
            if o != side:
                fetches[o, c].wait_send()
                returns[o, c].wait_send()
        stores[0, c].wait()
        stores[1, c].wait()


def on_device(queries, key_states, value_states, grads_out, doc_lengths, block_plan, needed):
    n = lax.axis_size("ctx")
    rows, width = queries.shape
    kv_width = key_states.shape[1]
    blocked = (rows // BLK, BLK, kv_width)
    key_count = rows + needed.shape[1] * BLK
    vmem = pl.BlockSpec(memory_space=pltpu.VMEM)
    smem = pl.BlockSpec(memory_space=pltpu.SMEM)
    anywhere = pl.BlockSpec(memory_space=pl.ANY)
    wide = jax.ShapeDtypeStruct((rows, width), jnp.bfloat16)
    narrow = jax.ShapeDtypeStruct((rows, kv_width), jnp.bfloat16)
    exchange = pltpu.VMEM((n, CHUNKS, BLK, WIDE), jnp.bfloat16)
    dma = pltpu.SemaphoreType.DMA
    return pl.pallas_call(
        functools.partial(kernel, n),
        out_shape=(wide, wide, narrow, narrow),
        in_specs=[anywhere, vmem, vmem, anywhere, smem, smem, smem],
        out_specs=(anywhere, anywhere, vmem, vmem),
        scratch_shapes=[pltpu.VMEM((rows, width), jnp.bfloat16)] * 4
        + [pltpu.VMEM((rows, kv_width), jnp.float32)] * 2
        + [pltpu.VMEM((key_count, rows), jnp.float32)]
        + [exchange] * 3
        + [pltpu.VMEM((n, BLK, WIDE), jnp.bfloat16)] * CHUNKS
        + [pltpu.VMEM((rows // BLK, BLK, WIDE), jnp.bfloat16)] * CHUNKS
        + [pltpu.VMEM((needed.shape[1], BLK, WIDE), jnp.bfloat16)] * (2 * CHUNKS)
        + [pltpu.VMEM((CHUNKS, rows // BLK, BLK, WIDE), jnp.bfloat16)]
        + [dma((n, CHUNKS))] * 4
        + [dma((2, CHUNKS))] * 2,
        compiler_params=pltpu.CompilerParams(collective_id=0, has_side_effects=True),
    )(
        queries,
        key_states.reshape(blocked),
        value_states.reshape(blocked),
        grads_out,
        doc_lengths,
        block_plan,
        needed,
    )


def solution(mesh):
    tokens = P(("grp", "ctx"), None)
    return jax.shard_map(
        on_device,
        mesh=mesh,
        in_specs=(tokens, tokens, tokens, tokens, P("grp"), P("grp"), P("grp", None)),
        out_specs=(tokens, tokens, tokens, tokens),
        check_vma=False,
    )
```

profile of v0, /device:TPU:0, one launch (start us, length us, event | category | flops | bytes accessed | tf_op | source)
XLA Modules:
  0.0 55.3 jit_solution(9543617171795174523)
XLA Ops:
  0.6 0.0 copy-start.3
  0.6 0.7 %copy-done.3 = s32[8,2]{0,1:T(2,128)S(1)} copy-done((s32[8,2]{0,1:T(2,128)S(1)}, s32[8,2]{0,1:T(2,128)}, u32[]{:S(2)}) %copy-start.3) | copy-done | bytes 88
  1.3 0.7 %copy.11.need_ref = s32[8,2]{1,0:T(8,128)} copy(s32[8,2]{0,1:T(2,128)S(1)} %copy-done.3) | data formatting | bytes 128 | tf_op args[6]
  2.0 48.3 %shard_map.102 = (bf16[128,4096]{1,0:T(8,128)(2,1)}, bf16[128,4096]{1,0:T(8,128)(2,1)}, bf16[128,512]{1,0:T(8,128)(2,1)}, bf16[128,512]{1,0:T(8,128)(2,1)}) custom-call(bf16[128,4096]{1,0:T(8,128)(2,1)} %q_hbm.1, bf16[2,64,512]{2,1,0:T(8,128)(2,1)} %bitcast.2, bf16[2,64,512]{2,1,0:T(8,128)(2,1)} %bitcast.3, bf16[128,4096]{1,0:T(8,128)(2,1)} %do_hbm.1, ...), custom_call_target="tpu_custom_call" | custom-call | tf_op jit(solution)/shard_map/pallas_call | solution.py:303
  50.3 0.0 copy-start
  50.3 2.4 %copy.16 = bf16[128,4096]{1,0:T(8,128)(2,1)} copy(bf16[128,4096]{1,0:T(8,128)(2,1)} %get-tuple-element.8) | data formatting | bytes 2097152
  52.7 0.0 copy-done
  52.7 0.0 copy-start.2
  52.7 1.0 %copy.17 = bf16[128,4096]{1,0:T(8,128)(2,1)} copy(bf16[128,4096]{1,0:T(8,128)(2,1)S(1)} %copy-done) | data formatting | bytes 2097152
  53.6 0.1 copy-done.2
  53.7 0.0 copy-start.1
  53.7 0.7 %copy.18 = bf16[128,512]{1,0:T(8,128)(2,1)} copy(bf16[128,512]{1,0:T(8,128)(2,1)S(1)} %copy-done.2) | data formatting | bytes 262144
  54.3 0.3 copy-done.1
  54.6 0.7 %copy.19 = bf16[128,512]{1,0:T(8,128)(2,1)} copy(bf16[128,512]{1,0:T(8,128)(2,1)S(1)} %copy-done.1) | data formatting | bytes 262144
Async XLA Ops:
  0.6 0.7 %copy-start.3 = (s32[8,2]{0,1:T(2,128)S(1)}, s32[8,2]{0,1:T(2,128)}, u32[]{:S(2)}) copy-start(s32[8,2]{0,1:T(2,128)} %param.13) | copy-start | bytes 196
  50.3 2.4 %copy-start = (bf16[128,4096]{1,0:T(8,128)(2,1)S(1)}, bf16[128,4096]{1,0:T(8,128)(2,1)}, u32[]{:S(2)}) copy-start(bf16[128,4096]{1,0:T(8,128)(2,1)} %get-tuple-element.9) | copy-start | bytes 3145732
  52.7 1.0 %copy-start.2 = (bf16[128,512]{1,0:T(8,128)(2,1)S(1)}, bf16[128,512]{1,0:T(8,128)(2,1)}, u32[]{:S(2)}) copy-start(bf16[128,512]{1,0:T(8,128)(2,1)} %get-tuple-element.10) | copy-start | bytes 393220
  53.7 1.0 %copy-start.1 = (bf16[128,512]{1,0:T(8,128)(2,1)S(1)}, bf16[128,512]{1,0:T(8,128)(2,1)}, u32[]{:S(2)}) copy-start(bf16[128,512]{1,0:T(8,128)(2,1)} %get-tuple-element.11) | copy-start | bytes 393220
where the time goes:
time: 55.5 us; the launch traced here: 55.3 us
  Pallas kernels  48.3 us (87%)
  local copies, waits for them, and re-layouts  6.35 us (11%)
  between operations  0.66 us (1%)
    pallas_call x1, Pallas kernels, on_device(): pl.pallas_call(functools.partial(kernel, n), out_shape=(wide, wide, narro...  48.3 us
    unnamed x13, local copies, waits for them, and re-layouts  6.35 us

commit v1 on v0

v1 whole, which is shorter than its diff:
```python
import functools
import math

import jax
import jax.numpy as jnp
from jax import lax
from jax.experimental import pallas as pl
from jax.experimental.pallas import tpu as pltpu
from jax.sharding import PartitionSpec as P

HEADS = 32
KV_HEADS = 4
HEAD_DIM = 128
BLK = 64
GROUP = HEADS // KV_HEADS
PIECES = 2 * KV_HEADS
PAIR = 2

masked_score = -1e30


def lane_count(n):
    lanes = 1
    for y in range(1, n + 1):
        if n % (2 * y) == 0 and 2 * y * y <= n:
            lanes = y
    return lanes


def matmul(a, b, contract):
    return lax.dot_general(
        a, b, ((contract[:1], contract[1:]), ((), ())), preferred_element_type=jnp.float32
    )


def kernel(n, q_hbm, k_hbm, v_hbm, do_hbm, doc_hbm, plan_hbm, need_hbm, *rest):
    out_ref, dq_ref, dk_ref, dv_ref = rest[:4]
    q_buf, do_buf, key_acc, value_acc, bias, doc_ref, plan_ref, need_ref = rest[4:12]
    rest = rest[12:]
    col, zs, zr, gz, ys, yr, ms, mr = (rest[i * PIECES : (i + 1) * PIECES] for i in range(8))
    (
        wide_sem,
        own_sem,
        table_sem,
        m_send,
        m_recv,
        yo_send,
        yo_recv,
        yr_send,
        yr_recv,
        z_send,
        z_recv,
        bz_send,
        bz_recv,
        by_send,
        by_recv,
        bm_send,
        bm_recv,
    ) = rest[8 * PIECES :]
    rows = q_buf.shape[0]
    own_blocks = rows // BLK
    listed_count = need_ref.shape[0]
    lanes = lane_count(n)
    columns = n // lanes
    half = columns // 2
    me = lax.axis_index("ctx")
    lane, column = lax.rem(me, lanes), me // lanes
    left = column < half
    place = jnp.where(left, column, columns - 1 - column)
    score_scale = 1.0 / math.sqrt(HEAD_DIM)
    chunk_cols = GROUP * HEAD_DIM

    def at_place(p, y):
        return jnp.where(left, p, columns - 1 - p) * lanes + y

    mirror = (columns - 1 - column) * lanes + lane
    lane_peer = [column * lanes + lax.rem(lane + o, lanes) for o in range(lanes)]
    place_peer = [at_place(lax.rem(place + o, half), lane) for o in range(half)]
    place_source = [at_place(lax.rem(place + half - o, half), lane) for o in range(half)]

    barrier = pltpu.get_barrier_semaphore()
    friends = [mirror] + lane_peer[1:] + place_peer[1:]
    for peer in friends:
        pl.semaphore_signal(
            barrier, inc=1, device_id={"ctx": peer}, device_id_type=pl.DeviceIdType.MESH
        )

    own_at = pl.ds(lane * 2 * own_blocks, own_blocks)
    relayed_at = pl.ds((lane * 2 + 1) * own_blocks, own_blocks)
    own_loads, loads = [], {}
    for p in range(PIECES):
        src = (k_hbm, v_hbm)[p % 2].at[:, :, pl.ds(p // 2 * HEAD_DIM, HEAD_DIM)]
        own_loads.append(pltpu.make_async_copy(src, col[p].at[own_at], own_sem.at[p]))
        own_loads[p].start()
    tables = [
        pltpu.make_async_copy(src, dst, table_sem.at[i])
        for i, (src, dst) in enumerate(
            ((doc_hbm, doc_ref), (plan_hbm, plan_ref), (need_hbm, need_ref))
        )
    ]
    for t in tables:
        t.start()
    for c in range(KV_HEADS):
        cols = pl.ds(c * chunk_cols, chunk_cols)
        for i, (src, dst) in enumerate(((q_hbm, q_buf), (do_hbm, do_buf))):
            loads[i, c] = pltpu.make_async_copy(
                src.at[:, cols], dst.at[:, cols], wide_sem.at[i, c]
            )
            loads[i, c].start()

    started = []

    def send(src, dst, sems, at, peer):
        copy = pltpu.make_async_remote_copy(
            src_ref=src,
            dst_ref=dst,
            send_sem=sems[0].at[at],
            recv_sem=sems[1].at[at],
            device_id={"ctx": peer},
            device_id_type=pl.DeviceIdType.MESH,
        )
        copy.start()
        started.append(copy)
        return copy

    for p in range(PIECES):
        own_loads[p].wait()
    pl.semaphore_wait(barrier, len(friends))
    to_mirror, to_lane, relays, to_place = [], [], {}, {}
    for p in range(PIECES):
        own = col[p].at[own_at]
        to_mirror.append(send(own, col[p].at[relayed_at], (m_send, m_recv), (p,), mirror))
    for p in range(PIECES):
        own = col[p].at[own_at]
        to_lane.append(
            [send(own, own, (yo_send, yo_recv), (p, o - 1), lane_peer[o]) for o in range(1, lanes)]
        )

    for t in tables:
        t.wait()
    ends, total = [], jnp.int32(0)
    for d in range(doc_ref.shape[0]):
        total = total + doc_ref[d]
        ends.append(total)

    def documents(at):
        doc = jnp.zeros_like(at)
        for end in ends:
            doc = doc + (at >= end).astype(jnp.int32)
        return doc

    key_row = lax.broadcasted_iota(jnp.int32, (BLK, rows), 0)
    query_col = lax.broadcasted_iota(jnp.int32, (BLK, rows), 1)
    query_local = query_col // BLK
    query_place = query_col
    for b in range(own_blocks):
        shift = (plan_ref[me * own_blocks + b] - b) * BLK
        query_place = jnp.where(query_local == b, query_col + shift, query_place)
    query_doc = documents(query_place)
    listed = [need_ref[j, me] for j in range(listed_count)]
    for s in range(own_blocks + listed_count):
        if s < own_blocks:
            block = me * own_blocks + s
            found = jnp.int32(0)
            for b in listed:
                found = jnp.where(b == block, 1, found)
            allowed = jnp.where(query_local == s, 1, found)
        else:
            block = listed[s - own_blocks]
            allowed = jnp.where(block // own_blocks == me, 0, jnp.ones_like(query_col))
        key_place = key_row + plan_ref[block] * BLK
        visible = (allowed > 0) & (documents(key_place) == query_doc) & (key_place <= query_place)
        bias[s * BLK : (s + 1) * BLK, :] = jnp.where(visible, 0.0, masked_score)

    def in_column(block):
        owner = block // own_blocks
        owner_left = owner // lanes < half
        side = jnp.where(owner_left == left, 0, 1)
        return ((owner % lanes) * 2 + side) * own_blocks + block % own_blocks

    def place_of(block):
        at = block // own_blocks // lanes
        return jnp.minimum(at, columns - 1 - at)

    chosen = [
        [in_column(need_ref[j, place_peer[o]]) for j in range(listed_count)] for o in range(half)
    ]
    slots = [lax.rem(place - place_of(b) + half, half) for b in listed]

    def relay(c):
        for p in (2 * c, 2 * c + 1):
            to_mirror[p].wait_recv()
            mine = col[p].at[relayed_at]
            relays[p] = [
                send(mine, mine, (yr_send, yr_recv), (p, o - 1), lane_peer[o])
                for o in range(1, lanes)
            ]

    def choose(c):
        for p in (2 * c, 2 * c + 1):
            for copy in to_lane[p] + relays[p]:
                copy.wait_recv()
            for o in list(range(1, half)) + [0]:
                for j in range(listed_count):
                    value = col[p][chosen[o][j]]
                    if o:
                        zs[p][o - 1, j] = value
                    else:
                        zr[p][0, j] = value
                if o:
                    to_place[p, o] = send(
                        zs[p].at[o - 1], zr[p].at[o], (z_send, z_recv), (p, o - 1), place_peer[o]
                    )

    exponent = score_scale * math.log2(math.e)
    state = {}

    def begin(c):
        loads[0, c].wait()
        loads[1, c].wait()
        whole = []
        for p in (2 * c, 2 * c + 1):
            for o in range(1, half):
                to_place[p, o].wait_recv()
            pieces = [col[p][lane * 2 * own_blocks + b] for b in range(own_blocks)]
            pieces += [zr[p][slots[j], j] for j in range(listed_count)]
            whole.append(jnp.concatenate(pieces, axis=0))
        keys, values = whole
        state[c] = dict(keys=keys, values=values, keys_t=keys.T, values_t=values.T)

    def attend(c, pair):
        s = state[c]
        heads = [
            slice(
                (c * GROUP + pair * PAIR + x) * HEAD_DIM,
                (c * GROUP + pair * PAIR + x + 1) * HEAD_DIM,
            )
            for x in range(PAIR)
        ]
        queries = jnp.concatenate([q_buf[:, at] for at in heads], axis=0)
        grads = jnp.concatenate([do_buf[:, at] for at in heads], axis=0)
        mask = bias[...]
        scores = matmul(s["keys"], queries, (1, 1)) + jnp.concatenate([mask] * PAIR, axis=1)
        highest = jnp.max(scores, axis=0, keepdims=True)
        weights = jnp.exp2((scores - highest) * exponent)
        weights = weights * (1.0 / jnp.sum(weights, axis=0, keepdims=True))
        low = weights.astype(jnp.bfloat16)
        attended = matmul(s["values_t"], low, (1, 0)).T.astype(jnp.bfloat16)
        prob_grads = matmul(s["values"], grads, (1, 1))
        delta = jnp.sum(weights * prob_grads, axis=0, keepdims=True)
        score_grads = (weights * (prob_grads - delta)).astype(jnp.bfloat16)
        query_grad = (matmul(s["keys_t"], score_grads, (1, 0)) * score_scale).T
        query_grad = query_grad.astype(jnp.bfloat16)
        for x, at in enumerate(heads):
            out_ref[:, at] = attended[x * rows : (x + 1) * rows]
            dq_ref[:, at] = query_grad[x * rows : (x + 1) * rows]
        more_keys = matmul(score_grads, queries, (1, 0))
        more_values = matmul(low, grads, (1, 0))
        if pair == 0:
            s["key_grad"], s["value_grad"] = more_keys, more_values
        else:
            s["key_grad"] = s["key_grad"] + more_keys
            s["value_grad"] = s["value_grad"] + more_values

    back_place, back_lane, back_mirror = {}, {}, {}

    def finish(c):
        s = state.pop(c)
        at = slice(c * HEAD_DIM, (c + 1) * HEAD_DIM)
        for p, acc, grad in (
            (2 * c + 1, value_acc, s["value_grad"]),
            (2 * c, key_acc, s["key_grad"] * score_scale),
        ):
            for j in range(listed_count):
                first = rows + j * BLK
                gz[p][0, j] = grad[first : first + BLK].astype(jnp.bfloat16)
            for o in range(1, half):
                back_place[p, o] = send(
                    gz[p].at[0], gz[p].at[o], (bz_send, bz_recv), (p, o - 1), place_peer[o]
                )
            acc[:, at] = grad[:rows]

    def block_of(side, y, b):
        at = column if side == 0 else columns - 1 - column
        return (at * lanes + y) * own_blocks + b

    def collect(p, side, y):
        targets = [block_of(side, y, b) for b in range(own_blocks)]
        zero = jnp.zeros((BLK, HEAD_DIM), jnp.float32)
        if half * listed_count <= 8:
            sums = [zero] * own_blocks
            for o in range(half):
                for j in range(listed_count):
                    block = need_ref[j, place_source[o]]
                    part = gz[p][o, j].astype(jnp.float32)
                    sums = [
                        x + jnp.where(block == t, part, 0.0)
                        for x, t in zip(sums, targets, strict=True)
                    ]
            return sums

        def add(i, sums):
            o, j = i // listed_count, i % listed_count
            block = need_ref[j, at_place(lax.rem(place + half - o, half), lane)]
            part = gz[p][o, j].astype(jnp.float32)
            return tuple(
                x + jnp.where(block == t, part, 0.0) for x, t in zip(sums, targets, strict=True)
            )

        return list(lax.fori_loop(0, half * listed_count, add, (zero,) * own_blocks))

    def spread(c):
        for p in (2 * c + 1, 2 * c):
            for o in range(1, half):
                back_place[p, o].wait_recv()
            for side in (1, 0):
                for o in range(1, lanes):
                    for b, x in enumerate(collect(p, side, lax.rem(lane + o, lanes))):
                        ys[p][o - 1, side, b] = x.astype(jnp.bfloat16)
                    back_lane[p, side, o] = send(
                        ys[p].at[o - 1, side],
                        yr[p].at[o - 1, side],
                        (by_send, by_recv),
                        (p, side, o - 1),
                        lane_peer[o],
                    )

    def reflect(c):
        for p in (2 * c + 1, 2 * c):
            for o in range(1, lanes):
                back_lane[p, 1, o].wait_recv()
            for b, x in enumerate(collect(p, 1, lane)):
                for o in range(1, lanes):
                    x = x + yr[p][o - 1, 1, b].astype(jnp.float32)
                ms[p][b] = x.astype(jnp.bfloat16)
            back_mirror[p] = send(ms[p], mr[p], (bm_send, bm_recv), (p,), mirror)

    def settle(c):
        at = slice(c * HEAD_DIM, (c + 1) * HEAD_DIM)
        for p, acc, result in ((2 * c + 1, value_acc, dv_ref), (2 * c, key_acc, dk_ref)):
            for o in range(1, lanes):
                back_lane[p, 0, o].wait_recv()
            sums = collect(p, 0, lane)
            back_mirror[p].wait_recv()
            for b, x in enumerate(sums):
                for o in range(1, lanes):
                    x = x + yr[p][o - 1, 0, b].astype(jnp.float32)
                x = x + mr[p][b].astype(jnp.float32) + acc[b * BLK : (b + 1) * BLK, at]
                result[b * BLK : (b + 1) * BLK, at] = x.astype(jnp.bfloat16)

    pairs = GROUP // PAIR
    last = KV_HEADS - 1
    relay(0)
    relay(1)
    choose(0)
    for c in range(2, last):
        relay(c)
        choose(c - 1)
    for c in range(KV_HEADS):
        begin(c)
        for pair in range(pairs):
            if pair == pairs // 2:
                if c == 0:
                    relay(last)
                if c == 1:
                    choose(last)
            attend(c, pair)
        finish(c)
        if c == 0:
            choose(last - 1)
        if c >= 1:
            spread(c - 1)
        if c >= 2:
            reflect(c - 2)
    settle(0)
    spread(last)
    reflect(last - 1)
    settle(1)
    reflect(last)
    for c in range(2, KV_HEADS):
        settle(c)
    for copy in started:
        copy.wait_send()


def write_out(*refs):
    sources, results, sem = refs[:4], refs[4:8], refs[8]
    copies = [
        pltpu.make_async_copy(src, dst, sem.at[i])
        for i, (src, dst) in enumerate(zip(sources, results, strict=True))
    ]
    for copy in copies:
        copy.start()
    for copy in copies:
        copy.wait()


def on_device(queries, key_states, value_states, grads_out, doc_lengths, block_plan, needed):
    n = lax.axis_size("ctx")
    rows, width = queries.shape
    kv_width = key_states.shape[1]
    own_blocks = rows // BLK
    blocked = (own_blocks, BLK, kv_width)
    listed = needed.shape[1]
    lanes = lane_count(n)
    half = n // lanes // 2
    vmem = pl.BlockSpec(memory_space=pltpu.VMEM)
    hbm = pl.BlockSpec(memory_space=pltpu.HBM)
    anywhere = pl.BlockSpec(memory_space=pl.ANY)
    wide = jax.ShapeDtypeStruct((rows, width), jnp.bfloat16)
    narrow = jax.ShapeDtypeStruct((rows, kv_width), jnp.bfloat16)
    results = (wide, wide, narrow, narrow)

    def store(*lead):
        return [pltpu.VMEM((*lead, BLK, HEAD_DIM), jnp.bfloat16)] * PIECES

    def sems(*shape):
        return [pltpu.SemaphoreType.DMA((PIECES, *shape))] * 2

    peers, others = max(lanes - 1, 1), max(half - 1, 1)
    parts = pl.pallas_call(
        functools.partial(kernel, n),
        out_shape=results,
        in_specs=[hbm] * 7,
        out_specs=(vmem,) * 4,
        scratch_shapes=[pltpu.VMEM((rows, width), jnp.bfloat16)] * 2
        + [pltpu.VMEM((rows, kv_width), jnp.float32)] * 2
        + [pltpu.VMEM((rows + listed * BLK, rows), jnp.float32)]
        + [pltpu.SMEM(x.shape, jnp.int32) for x in (doc_lengths, block_plan, needed.T)]
        + store(lanes * 2 * own_blocks)
        + store(others, listed)
        + store(half, listed)
        + store(half, listed)
        + store(peers, 2, own_blocks)
        + store(peers, 2, own_blocks)
        + store(own_blocks)
        + store(own_blocks)
        + [pltpu.SemaphoreType.DMA((2, KV_HEADS))]
        + [pltpu.SemaphoreType.DMA((PIECES,))]
        + [pltpu.SemaphoreType.DMA((3,))]
        + sems()
        + sems(peers)
        + sems(peers)
        + sems(others)
        + sems(others)
        + sems(2, peers)
        + sems(),
        compiler_params=pltpu.CompilerParams(
            collective_id=0, has_side_effects=True, vmem_limit_bytes=32 * 1024 * 1024
        ),
    )(
        *(
            pltpu.with_memory_space_constraint(x, pltpu.HBM)
            for x in (
                queries,
                key_states.reshape(blocked),
                value_states.reshape(blocked),
                grads_out,
                doc_lengths,
                block_plan,
                needed.T,
            )
        )
    )
    return pl.pallas_call(
        write_out,
        out_shape=results,
        in_specs=[vmem] * 4,
        out_specs=(anywhere,) * 4,
        scratch_shapes=[pltpu.SemaphoreType.DMA((4,))],
    )(*(pltpu.with_memory_space_constraint(x, pltpu.VMEM) for x in parts))


def solution(mesh):
    tokens = P(("grp", "ctx"), None)
    return jax.shard_map(
        on_device,
        mesh=mesh,
        in_specs=(tokens, tokens, tokens, tokens, P("grp"), P("grp"), P("grp", None)),
        out_specs=(tokens, tokens, tokens, tokens),
        check_vma=False,
    )
```

time: 55.5 us -> 47.1 us (0.85)
  local copies, waits for them, and re-layouts: 6.35 us -> 0 us
  Pallas kernels: 48.3 us -> 46.3 us
    unnamed x13 -> x0, local copies, waits for them, and re-layouts: 6.35 us -> none
    pallas_call x1 -> x2, Pallas kernels: 48.3 us -> 46.3 us  [the longest x1 44.9 us: on_device(): pl.pallas_call(functools.partial(kernel, n), out_shape=results, in_specs=...]
where the time goes in v1:
time: 47.1 us; the launch traced here: 47 us
  Pallas kernels  46.3 us (98%)
  between operations  0.64 us (1%)
    pallas_call x1, Pallas kernels, on_device(): pl.pallas_call(functools.partial(kernel, n), out_shape=results, in_specs=...  44.9 us
    pallas_call x1, Pallas kernels, on_device(): pl.pallas_call(write_out, out_shape=results, in_specs=[vmem] * 4, out_spe...  1.43 us

profile of v1, /device:TPU:0, one launch (start us, length us, event | category | flops | bytes accessed | tf_op | source)
XLA Modules:
  0.0 47.0 jit_solution(2978541789449695973)
XLA Ops:
  0.6 44.9 %shard_map.102 = (bf16[128,4096]{1,0:T(8,128)(2,1)S(1)}, bf16[128,4096]{1,0:T(8,128)(2,1)S(1)}, bf16[128,512]{1,0:T(8,128)(2,1)S(1)}, bf16[128,512]{1,0:T(8,128)(2,1)S(1)}) custom-call(bf16[128,4096]{1,0:T(8,128)(2,1)} %q_hbm.1, bf16[2,64,512]{2,1,0:T(8,128)(2,1)} %bitcast.3, bf16[2,64,512]{2,1,0:T(8,128)(2,1)} %bitcast.4, bf16[128,4096]{1,0:T(8,128)(2,1)} %do_hbm.1, ...), custom_call_target="tpu_custom_call" | custom-call | tf_op jit(solution)/shard_map/pallas_call | solution.py:421
  45.6 1.4 %shard_map.103 = (bf16[128,4096]{1,0:T(8,128)(2,1)}, bf16[128,4096]{1,0:T(8,128)(2,1)}, bf16[128,512]{1,0:T(8,128)(2,1)}, bf16[128,512]{1,0:T(8,128)(2,1)}) custom-call(bf16[128,4096]{1,0:T(8,128)(2,1)S(1)} %get-tuple-element.8.refs_0_, bf16[128,4096]{1,0:T(8,128)(2,1)S(1)} %get-tuple-element.9.refs_1_, bf16[128,512]{1,0:T(8,128)(2,1)S(1)} %get-tuple-element.10.refs_2_, ...), custom_call_target="tpu_custom_call" | custom-call | tf_op jit(solution)/shard_map/pallas_call | solution.py:465

commit v2 on v1

--- a/solution.py
+++ b/solution.py
@@ -36,7 +36,8 @@
 def kernel(n, q_hbm, k_hbm, v_hbm, do_hbm, doc_hbm, plan_hbm, need_hbm, *rest):
     out_ref, dq_ref, dk_ref, dv_ref = rest[:4]
     q_buf, do_buf, key_acc, value_acc, bias, doc_ref, plan_ref, need_ref = rest[4:12]
-    rest = rest[12:]
+    own_e, own_dp, own_o, stats, far_s, far_dp, low_buf, ds_buf = rest[12:20]
+    rest = rest[20:]
     col, zs, zr, gz, ys, yr, ms, mr = (rest[i * PIECES : (i + 1) * PIECES] for i in range(8))
     (
         wide_sem,
@@ -110,8 +111,8 @@
 
     started = []
 
-    def send(src, dst, sems, at, peer):
-        copy = pltpu.make_async_remote_copy(
+    def remote(src, dst, sems, at, peer):
+        return pltpu.make_async_remote_copy(
             src_ref=src,
             dst_ref=dst,
             send_sem=sems[0].at[at],
@@ -119,6 +120,9 @@
             device_id={"ctx": peer},
             device_id_type=pl.DeviceIdType.MESH,
         )
+
+    def send(src, dst, sems, at, peer):
+        copy = remote(src, dst, sems, at, peer)
         copy.start()
         started.append(copy)
         return copy
@@ -126,10 +130,24 @@
     for p in range(PIECES):
         own_loads[p].wait()
     pl.semaphore_wait(barrier, len(friends))
-    to_mirror, to_lane, relays, to_place = [], [], {}, {}
-    for p in range(PIECES):
-        own = col[p].at[own_at]
-        to_mirror.append(send(own, col[p].at[relayed_at], (m_send, m_recv), (p,), mirror))
+    to_lane, relays, to_place = [], {}, {}
+
+    to_mirror = [
+        remote(col[p].at[own_at], col[p].at[relayed_at], (m_send, m_recv), (p,), mirror)
+        for p in range(PIECES)
+    ]
+    innermost = place == half - 1
+
+    def cross(first, last):
+        for p in range(2 * first, 2 * last):
+            to_mirror[p].start()
+
+    cross(0, 1)
+    pl.when(innermost)(lambda: cross(1, KV_HEADS))
+    started += to_mirror
+
+    def release(c):
+        pl.when(jnp.logical_not(innermost))(lambda: cross(c, c + 1))
     for p in range(PIECES):
         own = col[p].at[own_at]
         to_lane.append(
@@ -213,54 +231,114 @@
                     )
 
     exponent = score_scale * math.log2(math.e)
+    span = PAIR * rows
     state = {}
 
-    def begin(c):
+    def heads_of(c, pair):
+        first = c * GROUP + pair * PAIR
+        return [slice((first + x) * HEAD_DIM, (first + x + 1) * HEAD_DIM) for x in range(PAIR)]
+
+    def stacked(ref, heads):
+        return jnp.concatenate([ref[:, at] for at in heads], axis=0)
+
+    def columns_of(c, pair):
+        first = (c * GROUP // PAIR + pair) * span
+        return slice(first, first + span)
+
+    def own_scores(c, pair):
+        heads, at = heads_of(c, pair), columns_of(c, pair)
+        mask = jnp.concatenate([bias[:rows]] * PAIR, axis=1)
+        own_e[:, at] = matmul(state[c]["own_keys"], stacked(q_buf, heads), (1, 1)) + mask
+        own_dp[:, at] = matmul(state[c]["own_values"], stacked(do_buf, heads), (1, 1))
+
+    def own_weights(c, pair):
+        at = columns_of(c, pair)
+        scores = own_e[:, at]
+        highest = jnp.max(scores, axis=0, keepdims=True)
+        weights = jnp.exp2((scores - highest) * exponent)
+        own_e[:, at] = weights
+        stats[0:1, at] = highest
+        stats[1:2, at] = jnp.sum(weights, axis=0, keepdims=True)
+        stats[2:3, at] = jnp.sum(weights * own_dp[:, at], axis=0, keepdims=True)
+        low_buf[pair, :rows] = weights.astype(jnp.bfloat16)
+
+    def own_output(c, pair):
+        own_o[:, columns_of(c, pair)] = matmul(
+            state[c]["own_values_t"], low_buf[pair, :rows], (1, 0)
+        )
+
+    pairs = GROUP // PAIR
+
+    def staged(c, stages):
+        for step in range(pairs + len(stages) - 1):
+            for i, stage in enumerate(stages):
+                if 0 <= step - i < pairs:
+                    stage(c, step - i)
+
+    def own_part(c):
         loads[0, c].wait()
         loads[1, c].wait()
-        whole = []
+        own_keys, own_values = (
+            jnp.concatenate([col[p][lane * 2 * own_blocks + b] for b in range(own_blocks)], axis=0)
+            for p in (2 * c, 2 * c + 1)
+        )
+        state[c] = dict(own_keys=own_keys, own_values=own_values, own_values_t=own_values.T)
+        staged(c, (own_scores, own_weights, own_output))
+
+    def listed_scores(c, pair):
+        heads = heads_of(c, pair)
+        mask = jnp.concatenate([bias[rows:]] * PAIR, axis=1)
+        far_s[pair] = matmul(state[c]["far_keys"], stacked(q_buf, heads), (1, 1)) + mask
+        far_dp[pair] = matmul(state[c]["far_values"], stacked(do_buf, heads), (1, 1))
+
+    def listed_weights(c, pair):
+        at = columns_of(c, pair)
+        scores, own_highest = far_s[pair], stats[0:1, at]
+        highest = jnp.maximum(jnp.max(scores, axis=0, keepdims=True), own_highest)
+        weights = jnp.exp2((scores - highest) * exponent)
+        own_scale = jnp.exp2((own_highest - highest) * exponent)
+        total = jnp.sum(weights, axis=0, keepdims=True) + own_scale * stats[1:2, at]
+        inverse = 1.0 / total
+        own_scale = own_scale * inverse
+        weights = weights * inverse
+        prob_grads = far_dp[pair]
+        delta = jnp.sum(weights * prob_grads, axis=0, keepdims=True) + own_scale * stats[2:3, at]
+        low_buf[pair, rows:] = weights.astype(jnp.bfloat16)
+        ds_buf[pair, rows:] = (weights * (prob_grads - delta)).astype(jnp.bfloat16)
+        weights = own_e[:, at] * own_scale
+        low_buf[pair, :rows] = weights.astype(jnp.bfloat16)
+        ds_buf[pair, :rows] = (weights * (own_dp[:, at] - delta)).astype(jnp.bfloat16)
+        stats[0:1, at] = own_scale
+
+    def results(c, pair):
+        at = columns_of(c, pair)
+        attended = matmul(state[c]["far_values_t"], low_buf[pair, rows:], (1, 0))
+        attended = attended + own_o[:, at] * stats[0:1, at]
+        query_grad = matmul(state[c]["keys_t"], ds_buf[pair], (1, 0)) * score_scale
+        for ref, value in ((out_ref, attended), (dq_ref, query_grad)):
+            value = value.astype(jnp.bfloat16).T
+            for x, head in enumerate(heads_of(c, pair)):
+                ref[:, head] = value[x * rows : (x + 1) * rows]
+
+    def begin(c):
+        far = []
         for p in (2 * c, 2 * c + 1):
             for o in range(1, half):
                 to_place[p, o].wait_recv()
-            pieces = [col[p][lane * 2 * own_blocks + b] for b in range(own_blocks)]
-            pieces += [zr[p][slots[j], j] for j in range(listed_count)]
-            whole.append(jnp.concatenate(pieces, axis=0))
-        keys, values = whole
-        state[c] = dict(keys=keys, values=values, keys_t=keys.T, values_t=values.T)
-
-    def attend(c, pair):
+            far.append(
+                jnp.concatenate([zr[p][slots[j], j] for j in range(listed_count)], axis=0)
+            )
         s = state[c]
-        heads = [
-            slice(
-                (c * GROUP + pair * PAIR + x) * HEAD_DIM,
-                (c * GROUP + pair * PAIR + x + 1) * HEAD_DIM,
-            )
-            for x in range(PAIR)
-        ]
-        queries = jnp.concatenate([q_buf[:, at] for at in heads], axis=0)
-        grads = jnp.concatenate([do_buf[:, at] for at in heads], axis=0)
-        mask = bias[...]
-        scores = matmul(s["keys"], queries, (1, 1)) + jnp.concatenate([mask] * PAIR, axis=1)
-        highest = jnp.max(scores, axis=0, keepdims=True)
-        weights = jnp.exp2((scores - highest) * exponent)
-        weights = weights * (1.0 / jnp.sum(weights, axis=0, keepdims=True))
-        low = weights.astype(jnp.bfloat16)
-        attended = matmul(s["values_t"], low, (1, 0)).T.astype(jnp.bfloat16)
-        prob_grads = matmul(s["values"], grads, (1, 1))
-        delta = jnp.sum(weights * prob_grads, axis=0, keepdims=True)
-        score_grads = (weights * (prob_grads - delta)).astype(jnp.bfloat16)
-        query_grad = (matmul(s["keys_t"], score_grads, (1, 0)) * score_scale).T
-        query_grad = query_grad.astype(jnp.bfloat16)
-        for x, at in enumerate(heads):
-            out_ref[:, at] = attended[x * rows : (x + 1) * rows]
-            dq_ref[:, at] = query_grad[x * rows : (x + 1) * rows]
-        more_keys = matmul(score_grads, queries, (1, 0))
-        more_values = matmul(low, grads, (1, 0))
-        if pair == 0:
-            s["key_grad"], s["value_grad"] = more_keys, more_values
-        else:
-            s["key_grad"] = s["key_grad"] + more_keys
-            s["value_grad"] = s["value_grad"] + more_values
+        s.update(far_keys=far[0], far_values=far[1], far_values_t=far[1].T)
+        s["keys_t"] = jnp.concatenate([s["own_keys"], far[0]], axis=0).T
+
+    def attend(c):
+        staged(c, (listed_scores, listed_weights, results))
+        s = state[c]
+        every = [head for pair in range(pairs) for head in heads_of(c, pair)]
+        for name, buf, ref in (("value_grad", low_buf, do_buf), ("key_grad", ds_buf, q_buf)):
+            weights = jnp.concatenate([buf[pair] for pair in range(pairs)], axis=1)
+            s[name] = matmul(weights, stacked(ref, every), (1, 0))
 
     back_place, back_lane, back_mirror = {}, {}, {}
 
@@ -309,21 +387,21 @@
 
         return list(lax.fori_loop(0, half * listed_count, add, (zero,) * own_blocks))
 
-    def spread(c):
+    def spread(c, side):
         for p in (2 * c + 1, 2 * c):
-            for o in range(1, half):
-                back_place[p, o].wait_recv()
-            for side in (1, 0):
-                for o in range(1, lanes):
-                    for b, x in enumerate(collect(p, side, lax.rem(lane + o, lanes))):
-                        ys[p][o - 1, side, b] = x.astype(jnp.bfloat16)
-                    back_lane[p, side, o] = send(
-                        ys[p].at[o - 1, side],
-                        yr[p].at[o - 1, side],
-                        (by_send, by_recv),
-                        (p, side, o - 1),
-                        lane_peer[o],
-                    )
+            if side:
+                for o in range(1, half):
+                    back_place[p, o].wait_recv()
+            for o in range(1, lanes):
+                for b, x in enumerate(collect(p, side, lax.rem(lane + o, lanes))):
+                    ys[p][o - 1, side, b] = x.astype(jnp.bfloat16)
+                back_lane[p, side, o] = send(
+                    ys[p].at[o - 1, side],
+                    yr[p].at[o - 1, side],
+                    (by_send, by_recv),
+                    (p, side, o - 1),
+                    lane_peer[o],
+                )
 
     def reflect(c):
         for p in (2 * c + 1, 2 * c):
@@ -348,37 +426,48 @@
                 x = x + mr[p][b].astype(jnp.float32) + acc[b * BLK : (b + 1) * BLK, at]
                 result[b * BLK : (b + 1) * BLK, at] = x.astype(jnp.bfloat16)
 
-    pairs = GROUP // PAIR
-    last = KV_HEADS - 1
-    relay(0)
-    relay(1)
-    choose(0)
-    for c in range(2, last):
-        relay(c)
-        choose(c - 1)
-    for c in range(KV_HEADS):
+    def compute(c):
         begin(c)
-        for pair in range(pairs):
-            if pair == pairs // 2:
-                if c == 0:
-                    relay(last)
-                if c == 1:
-                    choose(last)
-            attend(c, pair)
+        attend(c)
         finish(c)
-        if c == 0:
-            choose(last - 1)
-        if c >= 1:
-            spread(c - 1)
-        if c >= 2:
-            reflect(c - 2)
-    settle(0)
-    spread(last)
-    reflect(last - 1)
-    settle(1)
-    reflect(last)
-    for c in range(2, KV_HEADS):
-        settle(c)
+
+    def spread_mirrored(c):
+        spread(c, 1)
+
+    def spread_own(c):
+        spread(c, 0)
+
+    for stage, chunks in (
+        (own_part, (0, 1, 2)),
+        (relay, (0,)),
+        (release, (1, 2, 3)),
+        (own_part, (3,)),
+        (relay, (1,)),
+        (choose, (0,)),
+        (relay, (2,)),
+        (choose, (1,)),
+        (relay, (3,)),
+        (choose, (2,)),
+        (compute, (0,)),
+        (choose, (3,)),
+        (compute, (1,)),
+        (spread_mirrored, (0,)),
+        (compute, (2,)),
+        (spread_mirrored, (1,)),
+        (compute, (3,)),
+        (reflect, (0,)),
+        (spread_mirrored, (2,)),
+        (spread_own, (0,)),
+        (reflect, (1,)),
+        (spread_mirrored, (3,)),
+        (spread_own, (1,)),
+        (reflect, (2,)),
+        (spread_own, (2, 3)),
+        (reflect, (3,)),
+        (settle, (0, 1, 2, 3)),
+    ):
+        for c in chunks:
+            stage(c)
     for copy in started:
         copy.wait_send()
 
@@ -404,6 +493,7 @@
     listed = needed.shape[1]
     lanes = lane_count(n)
     half = n // lanes // 2
+    group_rows = HEADS * rows
     vmem = pl.BlockSpec(memory_space=pltpu.VMEM)
     hbm = pl.BlockSpec(memory_space=pltpu.HBM)
     anywhere = pl.BlockSpec(memory_space=pl.ANY)
@@ -427,6 +517,11 @@
         + [pltpu.VMEM((rows, kv_width), jnp.float32)] * 2
         + [pltpu.VMEM((rows + listed * BLK, rows), jnp.float32)]
         + [pltpu.SMEM(x.shape, jnp.int32) for x in (doc_lengths, block_plan, needed.T)]
+        + [pltpu.VMEM((rows, group_rows), jnp.float32)] * 2
+        + [pltpu.VMEM((HEAD_DIM, group_rows), jnp.float32)]
+        + [pltpu.VMEM((3, group_rows), jnp.float32)]
+        + [pltpu.VMEM((GROUP // PAIR, listed * BLK, PAIR * rows), jnp.float32)] * 2
+        + [pltpu.VMEM((GROUP // PAIR, rows + listed * BLK, PAIR * rows), jnp.bfloat16)] * 2
         + store(lanes * 2 * own_blocks)
         + store(others, listed)
         + store(half, listed)
@@ -446,7 +541,7 @@
         + sems(2, peers)
         + sems(),
         compiler_params=pltpu.CompilerParams(
-            collective_id=0, has_side_effects=True, vmem_limit_bytes=32 * 1024 * 1024
+            collective_id=0, has_side_effects=True, vmem_limit_bytes=48 * 1024 * 1024
         ),
     )(
         *(

time: 47.1 us -> 40.6 us (0.86)
  Pallas kernels: 46.3 us -> 39.8 us
    pallas_call x1, Pallas kernels: 44.9 us -> 38.4 us  [on_device(): pl.pallas_call(functools.partial(kernel, n), out_shape=results, in_specs=...]
where the time goes in v2:
time: 40.6 us; the launch traced here: 40.5 us
  Pallas kernels  39.8 us (98%)
  between operations  0.64 us (2%)
    pallas_call x1, Pallas kernels, on_device(): pl.pallas_call(functools.partial(kernel, n), out_shape=results, in_specs=...  38.4 us
    pallas_call x1, Pallas kernels, on_device(): pl.pallas_call(write_out, out_shape=results, in_specs=[vmem] * 4, out_spe...  1.43 us

profile of v2, /device:TPU:0, one launch (start us, length us, event | category | flops | bytes accessed | tf_op | source)
XLA Modules:
  0.0 40.5 jit_solution(14011486136520189774)
XLA Ops:
  0.6 38.4 %shard_map.102 = (bf16[128,4096]{1,0:T(8,128)(2,1)S(1)}, bf16[128,4096]{1,0:T(8,128)(2,1)S(1)}, bf16[128,512]{1,0:T(8,128)(2,1)S(1)}, bf16[128,512]{1,0:T(8,128)(2,1)S(1)}) custom-call(bf16[128,4096]{1,0:T(8,128)(2,1)} %q_hbm.1, bf16[2,64,512]{2,1,0:T(8,128)(2,1)} %bitcast.3, bf16[2,64,512]{2,1,0:T(8,128)(2,1)} %bitcast.4, bf16[128,4096]{1,0:T(8,128)(2,1)} %do_hbm.1, ...), custom_call_target="tpu_custom_call" | custom-call | tf_op jit(solution)/shard_map/pallas_call | solution.py:511
  39.0 1.4 %shard_map.103 = (bf16[128,4096]{1,0:T(8,128)(2,1)}, bf16[128,4096]{1,0:T(8,128)(2,1)}, bf16[128,512]{1,0:T(8,128)(2,1)}, bf16[128,512]{1,0:T(8,128)(2,1)}) custom-call(bf16[128,4096]{1,0:T(8,128)(2,1)S(1)} %get-tuple-element.8.refs_0_, bf16[128,4096]{1,0:T(8,128)(2,1)S(1)} %get-tuple-element.9.refs_1_, bf16[128,512]{1,0:T(8,128)(2,1)S(1)} %get-tuple-element.10.refs_2_, ...), custom_call_target="tpu_custom_call" | custom-call | tf_op jit(solution)/shard_map/pallas_call | solution.py:560
